TPU v7x, 32 devices: a whole 2x2x4 slice. The times are simulated.
32 devices in a mesh: mem: 8 (over z, y), dom: 4 (over x, core).
Axes of the slice: x: 2, y: 2, z: 4, core: 2. Of those that a mesh axis runs over, the one named last changes fastest.
Arguments:
- particle_states: float32 [64, 3, 256, 1024], P('mem', None, 'dom'), may hold values from -6 to 6
- coriolis: float32 [256], replicated, may hold values from -0.6 to 0.6
- observed_cells: int32 [4, 64, 512], P('dom', 'mem'), may hold values from 0 to 1023
- observed_values: float32 [4, 64, 512], P('dom', 'mem'), may hold values from -6 to 15
- resample_draws: int32 [4, 64, 8, 192], P('dom', 'mem'), may hold values from 0 to 63
Outputs:
- analysed: float32 [64, 3, 256, 1024], P('mem', None, 'dom')
All inputs are finite; a program needn't handle non-finite values.
Results may differ from a plain program's by a relative error of at most 0.0003.
Values sent between devices are 32-bit elements; how exact they have to be, the bound alone decides.
No kernel may reach another device: no remote copies, remote signals or barrier semaphores. Data moves between devices by JAX's collectives and lax.ppermute only.
A program may use at most 128 MiB of HBM per device.

v0:
```python
import jax
import jax.numpy as jnp
from jax import lax
from jax.sharding import PartitionSpec as P

LBLK = 128
LOC = 64
STEPS = 2


FLOW_FACTOR = 1.0
PRESSURE_FACTOR = 1.0
OBSERVATION_VARIANCE = 16.0
RELAXATION = 0.5
MERGE_FIRST = 0.75
BLEND_COEF_TWO = (13.0**0.5 + 1.0) / 8.0
MERGE_THIRD = -(13.0**0.5 - 1.0) / 8.0


def with_halo(array, sides, width):
    for axis, dim in sides:
        count, length = (lax.axis_size(axis), array.shape[dim])
        up = [(i, (i + 1) % count) for i in range(count - 1)]
        down = [(j, i) for i, j in up]
        last = lax.slice_in_dim(array, length - width, length, axis=dim)
        leading = lax.slice_in_dim(array, 0, width, axis=dim)
        before = lax.ppermute(last, axis, up)
        after = lax.ppermute(leading, axis, down)
        array = jnp.concatenate([before, array, after], axis=dim)
    return array


def along_east(quantity):
    return 0.5 * (jnp.roll(quantity, -1, axis=-1) - jnp.roll(quantity, 1, axis=-1))


def meridional_offset(quantity):
    border = jnp.zeros_like(quantity[..., :1, :])
    upper = jnp.concatenate([quantity[..., 1:, :], border], axis=-2)
    lower = jnp.concatenate([border, quantity[..., :-1, :]], axis=-2)
    return 0.5 * (upper - lower)


def advance(height, east_wind, north_wind, coriolis_col, inside):
    height_new = (
        height - FLOW_FACTOR * (along_east(east_wind) + meridional_offset(north_wind))
    ) * inside
    east_new = (
        east_wind - PRESSURE_FACTOR * along_east(height_new) + coriolis_col * north_wind
    ) * inside
    north_updated = (
        north_wind - PRESSURE_FACTOR * meridional_offset(height_new) - coriolis_col * east_wind
    ) * inside
    return (height_new, east_new, north_updated)


def tapering(cells, grid_width, block_cells, length):
    longitude = cells.astype(jnp.float32)
    tile_total = grid_width // block_cells
    centre = jnp.arange(tile_total).astype(jnp.float32) * block_cells + 0.5 * (block_cells - 1)
    distance = jnp.abs(longitude[..., :, None] - centre)
    distance = jnp.minimum(distance, grid_width - distance)
    return jnp.exp(-0.5 * (distance / length) ** 2)


def member_weights(heights, cells, values, block_cells, length):
    grid_width = heights.shape[-1]
    chosen_cells = (
        cells[:, None, :] == lax.broadcasted_iota(jnp.int32, (1, grid_width, 1), 1)
    ).astype(jnp.float32)
    observed = jnp.einsum("erl,rlo->reo", heights, chosen_cells, precision=lax.Precision.HIGHEST)
    misfit = (values[:, None, :] - observed) ** 2
    taper_weights = tapering(cells, grid_width, block_cells, length)
    likelihood = (
        -0.5
        / OBSERVATION_VARIANCE
        * jnp.einsum("reo,rob->rbe", misfit, taper_weights, precision=lax.Precision.HIGHEST)
    )
    largest = jnp.max(likelihood, axis=-1, keepdims=True)
    scaled = jnp.exp(likelihood - largest)
    return scaled / jnp.sum(scaled, axis=-1, keepdims=True)


def merge_members(members, weights, draws, block_cells):
    member_count, fields, count_of_rows, grid_width = members.shape
    tile_total = grid_width // block_cells
    split = draws.reshape(draws.shape[:-1] + (3, member_count))
    column = lax.broadcasted_iota(jnp.int32, (1, 1, 1, member_count), 3)
    picks = MERGE_FIRST * (split[:, :, 0, :, None] == column).astype(jnp.float32)
    picks = picks + BLEND_COEF_TWO * (split[:, :, 1, :, None] == column).astype(jnp.float32)
    picks = picks + MERGE_THIRD * (split[:, :, 2, :, None] == column).astype(jnp.float32)
    mixing_weights = (1.0 - RELAXATION) * weights[:, :, None, :] + RELAXATION * picks
    blocks = members.reshape(member_count, fields, count_of_rows, tile_total, block_cells)
    updated = jnp.einsum(
        "rbek,kfrbc->efrbc", mixing_weights, blocks, precision=lax.Precision.HIGHEST
    )
    return updated.reshape(member_count, fields, count_of_rows, grid_width)


def band_tables(coriolis, band_index, count_of_rows, margin):
    grid_rows = coriolis.shape[0]
    padded = jnp.pad(coriolis, (margin, margin))
    band_rows = lax.dynamic_slice_in_dim(
        padded, band_index * count_of_rows, count_of_rows + 2 * margin
    )
    position = (
        band_index * count_of_rows
        - margin
        + jnp.arange(count_of_rows + 2 * margin, dtype=jnp.int32)
    )
    inside = ((position >= 0) & (position < grid_rows)).astype(jnp.float32)
    return (band_rows[:, None], inside[:, None])


def body(particle_states, coriolis, observed_cells, observed_values, resample_draws):
    count_of_rows = particle_states.shape[2]
    band_index = lax.axis_index("dom")
    margin = 2 * STEPS
    coriolis_col, inside = band_tables(coriolis, band_index, count_of_rows, margin)
    padded = with_halo(particle_states, (("dom", 2),), 2 * STEPS)
    height, east_wind, north_wind = (padded[:, 0], padded[:, 1], padded[:, 2])
    for iteration_number in range(STEPS):
        height, east_wind, north_wind = advance(height, east_wind, north_wind, coriolis_col, inside)
    prior_estimates = jnp.stack(
        [
            height[:, margin : margin + count_of_rows],
            east_wind[:, margin : margin + count_of_rows],
            north_wind[:, margin : margin + count_of_rows],
        ],
        axis=1,
    )
    cells = observed_cells[0]
    values = observed_values[0]
    draws = resample_draws[0]
    gathered = lax.all_to_all(prior_estimates, "mem", split_axis=2, concat_axis=0, tiled=True)
    weights = member_weights(gathered[:, 0], cells, values, LBLK, LOC)
    updated = merge_members(gathered, weights, draws, LBLK)
    return lax.all_to_all(updated, "mem", split_axis=0, concat_axis=2, tiled=True)


def solution(mesh):
    return jax.shard_map(
        body,
        mesh=mesh,
        in_specs=(
            P("mem", None, "dom", None),
            P(),
            P("dom", "mem", None),
            P("dom", "mem", None),
            P("dom", "mem", None, None),
        ),
        out_specs=P("mem", None, "dom", None),
        check_vma=False,
    )
```

profile of v0, /device:TPU:0, one launch (start us, length us, event | category | flops | bytes accessed | tf_op | source)
XLA Modules:
  0.0 369.6 jit_solution(5722368060751329437)
XLA Ops:
  0.0 1.5 fusion.72
  1.8 2.4 collective-permute-start
  4.5 1.3 collective-permute-start.1
  6.1 6.4 %constant_dynamic-update-slice_fusion.1 = f32[8,3,72,1024]{3,0,2,1:T(8,128)S(1)} fusion(f32[8,3,72,1024]{3,0,2,1:T(8,128)S(1)} %constant_dynamic-update-slice_fusion.2, f32[8,3,64,1024]{3,2,1,0:T(8,128)} %param.5), kind=kLoop, calls=%fused_computation.83 | loop fusion | bytes 12582912
  12.5 0.4 slice_bitcast_fusion
  12.9 0.9 fusion.84
  14.0 0.6 fusion.82
  14.7 1.8 fusion.9
  16.5 0.8 fusion.81
  17.4 0.6 fusion.77
  18.1 2.2 subtract_multiply_fusion
  20.4 0.9 fusion.79
  21.5 0.6 fusion.76
  22.1 1.5 fusion.19
  23.6 1.0 fusion.74
  24.6 0.6 fusion.75
  25.6 2.8 fusion.30
  28.4 3.6 pad_maximum_fusion
  32.1 6.8 %all-to-all-start = ((f32[8,3,64,1024]{3,0,1,2:T(8,128)}), f32[8,3,64,1024]{3,0,1,2:T(8,128)}, u32[]{:S(2)}, u32[]{:S(2)}) async-start(f32[8,3,64,1024]{3,0,1,2:T(8,128)} %pad_maximum_fusion), calls=%async_computation | async-start | bytes 12582912 | tf_op jit(solution)/shard_map/all_to_all | solution.py:135
  39.1 136.5 %all-to-all-done = f32[8,3,64,1024]{3,0,1,2:T(8,128)} async-done(((f32[8,3,64,1024]{3,0,1,2:T(8,128)}), f32[8,3,64,1024]{3,0,1,2:T(8,128)}, u32[]{:S(2)}, u32[]{:S(2)}) %all-to-all-start) | async-done | bytes 6291488 | tf_op jit(solution)/shard_map/all_to_all | solution.py:135
  175.5 6.3 %copy.41 = f32[8,8,3,8,1024]{4,3,2,1,0:T(8,128)S(1)} copy(f32[8,8,3,8,1024]{4,1,2,3,0:T(8,128)} %bitcast.10) | data formatting | bytes 12582912 | tf_op jit(solution)/shard_map/all_to_all | solution.py:135
  181.9 0.2 slice.186
  182.1 0.5 copy-done.3
  182.6 6.8 %fusion.40 = f32[8,64,512]{2,1,0:T(8,128)S(1)} fusion(s32[8,512]{1,0:T(8,128)S(1)} %bitcast.78, f32[64,1,8,1024]{3,2,1,0:T(8,128)S(1)} %slice.186, f32[8,512]{1,0:T(8,128)S(1)} %bitcast.79), kind=kOutput, calls=%fused_computation.56 | convolution fusion | flops 3225944064 | bytes 3178496 | tf_op jit(solution)/shard_map/erl,rlo->reo/dot_general | solution.py:71
  189.4 1.0 convolution_multiply_fusion
  190.4 1.4 fusion.86
  191.9 1.5 copy.51
  193.5 14.0 %fusion.5 = f32[64,3,8,8,128]{4,0,1,3,2:T(8,128)S(1)} fusion(f32[64,3,8,8,128]{4,3,2,1,0:T(8,128)S(1)} %bitcast.73, s32[8,8,64]{2,1,0:T(8,128)S(1)} %bitcast.76, s32[8,8,64]{2,1,0:T(8,128)S(1)} %bitcast.77, s32[8,8,64]{2,1,0:T(8,128)S(1)} %bitcast.75, f32[8,8,64]{2,1,0:T(8,128)S(1)} %divide_multiply_fusion), kind=kOutput, calls=%fused_computation.8 | convolution fusion | flops 1210580992 | bytes 12648448 | tf_op jit(solution)/shard_map/rbek,kfrbc->efrbc/dot_general | solution.py:94
  207.5 6.3 %copy.45 = f32[64,3,8,8,128]{4,3,2,1,0:T(8,128)} copy(f32[64,3,8,8,128]{4,0,1,3,2:T(8,128)S(1)} %fusion.5) | data formatting | bytes 12582912 | tf_op jit(solution)/shard_map/rbek,kfrbc->efrbc/transpose | solution.py:94
  213.9 7.1 %reshape.37 = f32[64,3,8,1024]{3,2,1,0:T(8,128)} reshape(f32[64,3,8,8,128]{4,3,2,1,0:T(8,128)} %copy.45) | data formatting | bytes 12582912 | tf_op jit(solution)/shard_map/reshape | solution.py:97
  221.0 145.4 %all_to_all.36 = f32[64,3,8,1024]{3,2,1,0:T(8,128)S(1)} all-to-all(f32[64,3,8,1024]{3,2,1,0:T(8,128)} %reshape.37), channel_id=1, replica_groups=mesh['mem'=8,'dom'=4] {'mem'}, dimensions={0} | all-to-all | bytes 12582912 | tf_op jit(solution)/shard_map/all_to_all | solution.py:138
  366.4 3.3 copy.66
  (27 shorter events, 1.9 us)
Async XLA Ops:
  0.0 5.8 %copy-start.2 = (f32[256]{0:T(256)S(1)}, f32[256]{0:T(256)}, u32[]{:S(2)}) copy-start(f32[256]{0:T(256)} %param.6) | copy-start | bytes 3076
  1.8 4.2 %collective-permute-start = (f32[8,3,4,1024]{3,0,2,1:T(8,128)S(1)}, f32[8,3,4,1024]{3,0,2,1:T(8,128)S(1)}, u32[]{:S(2)}, u32[]{:S(2)}) collective-permute-start(f32[8,3,4,1024]{3,0,2,1:T(8,128)S(1)} %copy.64), channel_id=1, source_target_pairs={{0,1},{1,2},{2,3},{4,5},{5,6},{6,7},{8,9},{9,10},{10,11},{12,13},{... | collective-permute-start | bytes 1179656 | tf_op jit(solution)/shard_map/ppermute | solution.py:27
  4.5 8.0 %collective-permute-start.1 = (f32[8,3,4,1024]{3,0,2,1:T(8,128)S(1)}, f32[8,3,4,1024]{3,0,2,1:T(8,128)S(1)}, u32[]{:S(2)}, u32[]{:S(2)}) collective-permute-start(f32[8,3,4,1024]{3,0,2,1:T(8,128)S(1)} %copy.65), channel_id=1, source_target_pairs={{1,0},{2,1},{3,2},{5,4},{6,5},{7,6},{9,8},{10,9},{11,10},{13,12},{... | collective-permute-start | bytes 1179656 | tf_op jit(solution)/shard_map/ppermute | solution.py:28
  32.1 6.8 %copy-start = (s32[1,8,8,192]{3,2,1,0:T(8,128)S(1)}, s32[1,8,8,192]{3,2,1,0:T(8,128)}, u32[]{:S(2)}) copy-start(s32[1,8,8,192]{3,2,1,0:T(8,128)} %param.9) | copy-start | bytes 147460
  32.1 6.9 %copy-start.1 = (s32[1,8,512]{2,1,0:T(8,128)S(1)}, s32[1,8,512]{2,1,0:T(8,128)}, u32[]{:S(2)}) copy-start(s32[1,8,512]{2,1,0:T(8,128)} %param.7) | copy-start | bytes 49156
  32.1 143.5 %all-to-all-start = ((f32[8,3,64,1024]{3,0,1,2:T(8,128)}), f32[8,3,64,1024]{3,0,1,2:T(8,128)}, u32[]{:S(2)}, u32[]{:S(2)}) async-start(f32[8,3,64,1024]{3,0,1,2:T(8,128)} %pad_maximum_fusion), calls=%async_computation | async-start | bytes 12582912 | tf_op jit(solution)/shard_map/all_to_all | solution.py:135
  181.9 0.7 copy-start.3
where the time goes:
time: 370 us
  blocking collectives  145 us (39%)
  waiting for transfers between devices  136 us (37%)
  local copies, waits for them, and re-layouts  41.6 us (11%)
  matrix products  21.8 us (6%)
  other arithmetic  13.6 us (4%)
  starting transfers between devices  10.5 us (3%)
    all_to_all x1, blocking collectives, body(): lax.all_to_all(updated, 'mem', split_axis=0, concat_axis=2, tiled=True)  145 us
    all_to_all x1, waiting for transfers between devices, body(): lax.all_to_all(prior_estimates, 'mem', split_axis=2, concat_axis=0, tiled...  136 us
    dot_general x1, matrix products, merge_members(): jnp.einsum('rbek,kfrbc->efrbc', mixing_weights, blocks, precision=lax.Pre...  14 us
    unnamed x13, local copies, waits for them, and re-layouts  8.95 us
  transfers between devices with their start and end apart: 3, of which 1 were waited for; matrix products, arithmetic and copies ran while one was open for 2% of the time, Pallas kernels for 0%

commit v1 on v0

--- a/solution.py
+++ b/solution.py
@@ -81,20 +81,21 @@
     return scaled / jnp.sum(scaled, axis=-1, keepdims=True)
 
 
-def merge_members(members, weights, draws, block_cells):
-    member_count, fields, count_of_rows, grid_width = members.shape
-    tile_total = grid_width // block_cells
+def mixing_matrix(weights, draws):
+    member_count = weights.shape[-1]
     split = draws.reshape(draws.shape[:-1] + (3, member_count))
     column = lax.broadcasted_iota(jnp.int32, (1, 1, 1, member_count), 3)
     picks = MERGE_FIRST * (split[:, :, 0, :, None] == column).astype(jnp.float32)
     picks = picks + BLEND_COEF_TWO * (split[:, :, 1, :, None] == column).astype(jnp.float32)
     picks = picks + MERGE_THIRD * (split[:, :, 2, :, None] == column).astype(jnp.float32)
-    mixing_weights = (1.0 - RELAXATION) * weights[:, :, None, :] + RELAXATION * picks
-    blocks = members.reshape(member_count, fields, count_of_rows, tile_total, block_cells)
-    updated = jnp.einsum(
-        "rbek,kfrbc->efrbc", mixing_weights, blocks, precision=lax.Precision.HIGHEST
-    )
-    return updated.reshape(member_count, fields, count_of_rows, grid_width)
+    return (1.0 - RELAXATION) * weights[:, :, None, :] + RELAXATION * picks
+
+
+def merge_field(members, mixing, block_cells):
+    member_count, count_of_rows, grid_width = members.shape
+    blocks = members.reshape(member_count, count_of_rows, grid_width // block_cells, block_cells)
+    updated = jnp.einsum("rbek,krbc->erbc", mixing, blocks, precision=lax.Precision.HIGHEST)
+    return updated.reshape(member_count, count_of_rows, grid_width)
 
 
 def band_tables(coriolis, band_index, count_of_rows, margin):
@@ -121,21 +122,24 @@
     height, east_wind, north_wind = (padded[:, 0], padded[:, 1], padded[:, 2])
     for iteration_number in range(STEPS):
         height, east_wind, north_wind = advance(height, east_wind, north_wind, coriolis_col, inside)
-    prior_estimates = jnp.stack(
-        [
-            height[:, margin : margin + count_of_rows],
-            east_wind[:, margin : margin + count_of_rows],
-            north_wind[:, margin : margin + count_of_rows],
-        ],
-        axis=1,
-    )
     cells = observed_cells[0]
     values = observed_values[0]
     draws = resample_draws[0]
-    gathered = lax.all_to_all(prior_estimates, "mem", split_axis=2, concat_axis=0, tiled=True)
-    weights = member_weights(gathered[:, 0], cells, values, LBLK, LOC)
-    updated = merge_members(gathered, weights, draws, LBLK)
-    return lax.all_to_all(updated, "mem", split_axis=0, concat_axis=2, tiled=True)
+    gathered = [
+        lax.all_to_all(
+            field[:, margin : margin + count_of_rows], "mem", split_axis=1, concat_axis=0, tiled=True
+        )
+        for field in (height, east_wind, north_wind)
+    ]
+    weights = member_weights(gathered[0], cells, values, LBLK, LOC)
+    mixing = mixing_matrix(weights, draws)
+    returned = [
+        lax.all_to_all(
+            merge_field(field, mixing, LBLK), "mem", split_axis=0, concat_axis=1, tiled=True
+        )
+        for field in gathered
+    ]
+    return jnp.stack(returned, axis=1)
 
 
 def solution(mesh):

time: 370 us -> 351 us (0.949)
  blocking collectives: 145 us -> 54.6 us
  waiting for transfers between devices: 136 us -> 172 us
  starting transfers between devices: 10.5 us -> 26.7 us
  local copies, waits for them, and re-layouts: 41.6 us -> 53.9 us
  matrix products: 21.8 us -> 30.4 us
    all_to_all x1, blocking collectives: 145 us -> 54.6 us  [body(): lax.all_to_all(field[:, margin:margin + count_of_rows], 'mem', split_axis...]
    all_to_all x1 -> x5, waiting for transfers between devices: 136 us -> 172 us  [the longest x3 109 us: body(): lax.all_to_all(merge_field(field, mixing, LBLK), 'mem', split_axis=0, con...]
    all_to_all x1 -> x5, starting transfers between devices: 6.78 us -> 23 us  [the longest x3 12.5 us: body(): lax.all_to_all(merge_field(field, mixing, LBLK), 'mem', split_axis=0, con...]
    dot_general x1 -> x3, matrix products: 14 us -> 22.5 us  [merge_field(): jnp.einsum('rbek,krbc->erbc', mixing, blocks, precision=lax.Precision.HIG...]
    another operation x2 -> x1, other arithmetic: 6.47 us -> 1.11 us  [body(): return jnp.stack(returned, axis=1)]
    unnamed x13 -> x27, local copies, waits for them, and re-layouts: 8.95 us -> 13.2 us
    mul x1 -> x2, other arithmetic: 0.08 us -> 3.92 us  [the longest x1 3.78 us: advance(): (east_wind - PRESSURE_FACTOR * along_east(height_new) + coriolis_col * no...]
    all_to_all x2 -> x6, local copies, waits for them, and re-layouts: 9.62 us -> 13.3 us  [the longest x3 6.77 us: body(): lax.all_to_all(field[:, margin:margin + count_of_rows], 'mem', split_axis...]
  transfers between devices with their start and end apart: 3 -> 7, of which waited for: 1 -> 5; matrix products, arithmetic and copies ran while one was open for 2% -> 21% of each run, Pallas kernels for 0% -> 0%
where the time goes in v1:
time: 351 us; the launch traced here: 350 us
  waiting for transfers between devices  172 us (49%)
  blocking collectives  54.6 us (16%)
  local copies, waits for them, and re-layouts  53.9 us (15%)
  matrix products  30.4 us (9%)
  starting transfers between devices  26.7 us (8%)
  other arithmetic  11.6 us (3%)
    all_to_all x3, waiting for transfers between devices, body(): lax.all_to_all(merge_field(field, mixing, LBLK), 'mem', split_axis=0, con...  109 us
    all_to_all x2, waiting for transfers between devices, body(): lax.all_to_all(field[:, margin:margin + count_of_rows], 'mem', split_axis...  62.7 us
    all_to_all x1, blocking collectives, body(): lax.all_to_all(field[:, margin:margin + count_of_rows], 'mem', split_axis...  54.6 us
    dot_general x3, matrix products, merge_field(): jnp.einsum('rbek,krbc->erbc', mixing, blocks, precision=lax.Precision.HIG...  22.5 us
    unnamed x27, local copies, waits for them, and re-layouts  13.2 us
    all_to_all x3, starting transfers between devices, body(): lax.all_to_all(merge_field(field, mixing, LBLK), 'mem', split_axis=0, con...  12.5 us
    all_to_all x2, starting transfers between devices, body(): lax.all_to_all(field[:, margin:margin + count_of_rows], 'mem', split_axis...  10.4 us
    reshape x3, local copies, waits for them, and re-layouts, merge_field(): return updated.reshape(member_count, count_of_rows, grid_width)  7.03 us
  transfers between devices with their start and end apart: 7, of which 5 were waited for; matrix products, arithmetic and copies ran while one was open for 21% of the time, Pallas kernels for 0%

profile of v1, /device:TPU:0, one launch (start us, length us, event | category | flops | bytes accessed | tf_op | source)
XLA Modules:
  0.0 349.7 jit_solution(9708759110134886916)
XLA Ops:
  0.0 1.5 fusion.105
  1.8 2.4 collective-permute-start
  5.9 6.4 %constant_dynamic-update-slice_fusion.1 = f32[8,3,72,1024]{3,0,2,1:T(8,128)S(1)} fusion(f32[8,3,72,1024]{3,0,2,1:T(8,128)S(1)} %constant_dynamic-update-slice_fusion.2, f32[8,3,64,1024]{3,2,1,0:T(8,128)} %param.5), kind=kLoop, calls=%fused_computation.102 | loop fusion | bytes 12582912
  14.5 1.7 fusion.4
  17.9 2.1 subtract_multiply_fusion
  23.0 1.5 fusion.14
  24.5 1.5 slice.167
  26.1 6.7 %all-to-all-start = ((f32[8,64,1024]{2,0,1:T(8,128)}), f32[8,64,1024]{2,0,1:T(8,128)}, u32[]{:S(2)}, u32[]{:S(2)}) async-start(f32[8,64,1024]{2,0,1:T(8,128)} %slice.167), calls=%async_computation | async-start | bytes 4194304 | tf_op jit(solution)/shard_map/all_to_all | solution.py:129
  36.0 3.8 %fusion.23 = (f32[8,64,1024]{2,0,1:T(8,128)S(1)}, f32[8,64,1024]{2,0,1:T(8,128)}) fusion(f32[8,72,1]{2,0,1:T(8,128)S(1)} %get-tuple-element.14, f32[8,72,1023]{2,0,1:T(8,128)S(1)} %get-tuple-element.16, f32[8,72,1023]{2,0,1:T(8,128)S(1)} %get-tuple-element.15, f32[8,72,1]{2,0,1:T(8,128)S(1)} %get-tuple-element.13, f32[8,72,1024]{2,0,1:T(8,128)S(1)} %copy-done.3, ...), kind=kLoop, calls=%fused_computation.37 | loop fusion | flops 7340032 | bytes 17760768 | tf_op jit(solution)/shard_map/mul | solution.py:48
  39.8 40.2 %all-to-all-done = f32[8,64,1024]{2,0,1:T(8,128)} async-done(((f32[8,64,1024]{2,0,1:T(8,128)}), f32[8,64,1024]{2,0,1:T(8,128)}, u32[]{:S(2)}, u32[]{:S(2)}) %all-to-all-start) | async-done | bytes 2097184 | tf_op jit(solution)/shard_map/all_to_all | solution.py:129
  80.0 54.6 %all_to_all.93 = f32[8,64,1024]{2,0,1:T(8,128)} all-to-all(f32[8,64,1024]{2,0,1:T(8,128)S(1)} %get-tuple-element.11), channel_id=1, replica_groups=mesh['mem'=8,'dom'=4] {'mem'}, dimensions={1} | all-to-all | bytes 4194304 | tf_op jit(solution)/shard_map/all_to_all | solution.py:129
  134.6 3.8 %all-to-all-start.4 = ((f32[8,64,1024]{2,0,1:T(8,128)}), f32[8,64,1024]{2,0,1:T(8,128)S(1)}, u32[]{:S(2)}, u32[]{:S(2)}) async-start(f32[8,64,1024]{2,0,1:T(8,128)} %get-tuple-element.12), calls=%async_computation.4 | async-start | bytes 4194304 | tf_op jit(solution)/shard_map/all_to_all | solution.py:129
  138.6 2.8 copy.40
  142.1 6.8 %fusion.43 = f32[8,64,512]{2,1,0:T(8,128)S(1)} fusion(s32[8,512]{1,0:T(8,128)S(1)} %bitcast.108, f32[64,8,1024]{2,1,0:T(8,128)S(1)} %bitcast.93, f32[8,512]{1,0:T(8,128)S(1)} %bitcast.109), kind=kOutput, calls=%fused_computation.57 | convolution fusion | flops 3225944064 | bytes 3178496 | tf_op jit(solution)/shard_map/erl,rlo->reo/dot_general | solution.py:71
  151.3 7.5 %fusion.31 = f32[64,8,8,128]{3,0,2,1:T(8,128)S(1)} fusion(f32[64,8,8,128]{3,2,1,0:T(8,128)S(1)} %copy.89, s32[8,8,64]{2,1,0:T(8,128)S(1)} %bitcast.102, s32[8,8,64]{2,1,0:T(8,128)S(1)} %bitcast.105, s32[8,8,64]{2,1,0:T(8,128)S(1)} %bitcast.99, f32[8,8,64]{2,1,0:T(8,128)S(1)} %divide_multiply_fusion), kind=kOutput, calls=%fused_computation.53 | convolution fusion | flops 405274624 | bytes 4259840 | tf_op jit(solution)/shard_map/rbek,krbc->erbc/dot_general | solution.py:97
  158.9 2.6 copy.44
  161.4 2.8 reshape.54
  164.2 22.5 %all-to-all-done.4 = f32[8,64,1024]{2,0,1:T(8,128)S(1)} async-done(((f32[8,64,1024]{2,0,1:T(8,128)}), f32[8,64,1024]{2,0,1:T(8,128)S(1)}, u32[]{:S(2)}, u32[]{:S(2)}) %all-to-all-start.4) | async-done | bytes 2097184 | tf_op jit(solution)/shard_map/all_to_all | solution.py:129
  186.7 4.6 %all-to-all-start.1 = ((f32[64,8,1024]{2,1,0:T(8,128)}), f32[64,8,1024]{2,1,0:T(8,128)}, u32[]{:S(2)}, u32[]{:S(2)}) async-start(f32[64,8,1024]{2,1,0:T(8,128)} %reshape.54), calls=%async_computation.1 | async-start | bytes 4194304 | tf_op jit(solution)/shard_map/all_to_all | solution.py:137
  191.3 2.8 copy.46
  194.5 7.5 %fusion.34 = f32[64,8,8,128]{3,0,2,1:T(8,128)S(1)} fusion(f32[64,8,8,128]{3,2,1,0:T(8,128)S(1)} %copy.88, s32[8,8,64]{2,1,0:T(8,128)S(1)} %bitcast.103, s32[8,8,64]{2,1,0:T(8,128)S(1)} %bitcast.106, s32[8,8,64]{2,1,0:T(8,128)S(1)} %bitcast.100, f32[8,8,64]{2,1,0:T(8,128)S(1)} %divide_multiply_fusion), kind=kOutput, calls=%fused_computation.54 | convolution fusion | flops 405274624 | bytes 4259840 | tf_op jit(solution)/shard_map/rbek,krbc->erbc/dot_general | solution.py:97
  202.0 2.5 copy.48
  204.6 2.8 reshape.56
  207.4 31.6 %all-to-all-done.1 = f32[64,8,1024]{2,1,0:T(8,128)} async-done(((f32[64,8,1024]{2,1,0:T(8,128)}), f32[64,8,1024]{2,1,0:T(8,128)}, u32[]{:S(2)}, u32[]{:S(2)}) %all-to-all-start.1) | async-done | bytes 2097184 | tf_op jit(solution)/shard_map/all_to_all | solution.py:137
  239.0 4.4 %all-to-all-start.3 = ((f32[64,8,1024]{2,1,0:T(8,128)}), f32[64,8,1024]{2,1,0:T(8,128)}, u32[]{:S(2)}, u32[]{:S(2)}) async-start(f32[64,8,1024]{2,1,0:T(8,128)} %reshape.56), calls=%async_computation.3 | async-start | bytes 4194304 | tf_op jit(solution)/shard_map/all_to_all | solution.py:137
  245.0 7.5 %fusion.37 = f32[64,8,8,128]{3,0,2,1:T(8,128)S(1)} fusion(f32[64,8,8,128]{3,2,1,0:T(8,128)S(1)} %copy.87, s32[8,8,64]{2,1,0:T(8,128)S(1)} %bitcast.104, s32[8,8,64]{2,1,0:T(8,128)S(1)} %bitcast.107, s32[8,8,64]{2,1,0:T(8,128)S(1)} %bitcast.101, f32[8,8,64]{2,1,0:T(8,128)S(1)} %divide_multiply_fusion), kind=kOutput, calls=%fused_computation.55 | convolution fusion | flops 405274624 | bytes 4259840 | tf_op jit(solution)/shard_map/rbek,krbc->erbc/dot_general | solution.py:97
  255.3 35.8 %all-to-all-done.3 = f32[64,8,1024]{2,1,0:T(8,128)} async-done(((f32[64,8,1024]{2,1,0:T(8,128)}), f32[64,8,1024]{2,1,0:T(8,128)}, u32[]{:S(2)}, u32[]{:S(2)}) %all-to-all-start.3) | async-done | bytes 2097184 | tf_op jit(solution)/shard_map/all_to_all | solution.py:137
  291.0 3.6 %all-to-all-start.5 = ((f32[64,8,1024]{2,1,0:T(8,128)}), f32[64,8,1024]{2,1,0:T(8,128)S(1)}, u32[]{:S(2)}, u32[]{:S(2)}) async-start(f32[64,8,1024]{2,1,0:T(8,128)} %reshape.58), calls=%async_computation.5 | async-start | bytes 4194304 | tf_op jit(solution)/shard_map/all_to_all | solution.py:137
  294.7 3.2 copy.92
  297.9 3.2 copy.91
  301.1 42.0 %all-to-all-done.5 = f32[64,8,1024]{2,1,0:T(8,128)S(1)} async-done(((f32[64,8,1024]{2,1,0:T(8,128)}), f32[64,8,1024]{2,1,0:T(8,128)S(1)}, u32[]{:S(2)}, u32[]{:S(2)}) %all-to-all-start.5) | async-done | bytes 2097184 | tf_op jit(solution)/shard_map/all_to_all | solution.py:137
  346.4 3.3 copy.54
  (59 shorter events, 23.3 us)
Async XLA Ops:
  0.0 5.8 %copy-start.8 = (f32[256]{0:T(256)S(1)}, f32[256]{0:T(256)}, u32[]{:S(2)}) copy-start(f32[256]{0:T(256)} %param.6) | copy-start | bytes 3076
  1.8 4.1 %collective-permute-start = (f32[8,3,4,1024]{3,0,2,1:T(8,128)S(1)}, f32[8,3,4,1024]{3,0,2,1:T(8,128)S(1)}, u32[]{:S(2)}, u32[]{:S(2)}) collective-permute-start(f32[8,3,4,1024]{3,0,2,1:T(8,128)S(1)} %copy.85), channel_id=1, source_target_pairs={{0,1},{1,2},{2,3},{4,5},{5,6},{6,7},{8,9},{9,10},{10,11},{12,13},{... | collective-permute-start | bytes 1179656 | tf_op jit(solution)/shard_map/ppermute | solution.py:27
  4.5 7.9 %collective-permute-start.1 = (f32[8,3,4,1024]{3,0,2,1:T(8,128)S(1)}, f32[8,3,4,1024]{3,0,2,1:T(8,128)S(1)}, u32[]{:S(2)}, u32[]{:S(2)}) collective-permute-start(f32[8,3,4,1024]{3,0,2,1:T(8,128)S(1)} %copy.86), channel_id=1, source_target_pairs={{1,0},{2,1},{3,2},{5,4},{6,5},{7,6},{9,8},{10,9},{11,10},{13,12},{... | collective-permute-start | bytes 1179656 | tf_op jit(solution)/shard_map/ppermute | solution.py:28
  20.0 1.4 copy-start
  20.0 2.2 copy-start.2
  26.1 53.9 %all-to-all-start = ((f32[8,64,1024]{2,0,1:T(8,128)}), f32[8,64,1024]{2,0,1:T(8,128)}, u32[]{:S(2)}, u32[]{:S(2)}) async-start(f32[8,64,1024]{2,0,1:T(8,128)} %slice.167), calls=%async_computation | async-start | bytes 4194304 | tf_op jit(solution)/shard_map/all_to_all | solution.py:129
  33.6 1.7 copy-start.1
  33.6 2.4 copy-start.3
  134.6 3.8 %copy-start.6 = (s32[1,8,8,192]{3,2,1,0:T(8,128)S(1)}, s32[1,8,8,192]{3,2,1,0:T(8,128)}, u32[]{:S(2)}) copy-start(s32[1,8,8,192]{3,2,1,0:T(8,128)} %param.9) | copy-start | bytes 147460
  134.6 3.9 %copy-start.7 = (s32[1,8,512]{2,1,0:T(8,128)S(1)}, s32[1,8,512]{2,1,0:T(8,128)}, u32[]{:S(2)}) copy-start(s32[1,8,512]{2,1,0:T(8,128)} %param.7) | copy-start | bytes 49156
  134.6 52.1 %all-to-all-start.4 = ((f32[8,64,1024]{2,0,1:T(8,128)}), f32[8,64,1024]{2,0,1:T(8,128)S(1)}, u32[]{:S(2)}, u32[]{:S(2)}) async-start(f32[8,64,1024]{2,0,1:T(8,128)} %get-tuple-element.12), calls=%async_computation.4 | async-start | bytes 4194304 | tf_op jit(solution)/shard_map/all_to_all | solution.py:129
  141.4 0.7 copy-start.9
  186.7 52.3 %all-to-all-start.1 = ((f32[64,8,1024]{2,1,0:T(8,128)}), f32[64,8,1024]{2,1,0:T(8,128)}, u32[]{:S(2)}, u32[]{:S(2)}) async-start(f32[64,8,1024]{2,1,0:T(8,128)} %reshape.54), calls=%async_computation.1 | async-start | bytes 4194304 | tf_op jit(solution)/shard_map/all_to_all | solution.py:137
  239.0 52.1 %all-to-all-start.3 = ((f32[64,8,1024]{2,1,0:T(8,128)}), f32[64,8,1024]{2,1,0:T(8,128)}, u32[]{:S(2)}, u32[]{:S(2)}) async-start(f32[64,8,1024]{2,1,0:T(8,128)} %reshape.56), calls=%async_computation.3 | async-start | bytes 4194304 | tf_op jit(solution)/shard_map/all_to_all | solution.py:137
  291.0 52.0 %all-to-all-start.5 = ((f32[64,8,1024]{2,1,0:T(8,128)}), f32[64,8,1024]{2,1,0:T(8,128)S(1)}, u32[]{:S(2)}, u32[]{:S(2)}) async-start(f32[64,8,1024]{2,1,0:T(8,128)} %reshape.58), calls=%async_computation.5 | async-start | bytes 4194304 | tf_op jit(solution)/shard_map/all_to_all | solution.py:137
  343.1 1.6 copy-start.4
  343.1 2.2 copy-start.5
